TPU v7x, 32 devices: a whole 2x2x4 slice. The times are simulated.
32 devices in a mesh: row: 4 (over z), col: 8 (over y, x, core).
Axes of the slice: x: 2, y: 2, z: 4, core: 2. Of those that a mesh axis runs over, the one named last changes fastest.
Arguments:
- eigvecs: bfloat16 [40960, 2048], P('row', 'col'), may hold values from -0.125 to 0.125
- reflectors: bfloat16 [2, 40960, 128], P(None, 'row'), may hold values from -6 to 6
- factors: float32 [2, 128, 128], replicated, may hold values from -0.00024414062 to 0.00024414062
- frequencies: float32 [2048], replicated, may hold values from 0.3 to 3
- region_blocks: int32 [72], P('row'), may hold values from 0 to 319, as said below
Outputs:
- covariance: float32 [9216, 9216], P('row', 'col')
Inputs may be any that keep to these rules, and one draw needn't show every extreme that they name: `region_blocks`: the 72 block numbers are distinct and ascending; exactly 18 of them lie in each consecutive run of 80 block numbers.
All inputs are finite; a program needn't handle non-finite values.
Results may differ from a plain program's by a relative error of at most 0.004.
Values may be sent and summed in bfloat16 or wider, within the bound.
A program may use at most 128 MiB of HBM per device.

v0:
```python
import jax
import jax.numpy as jnp
from jax import lax
from jax.sharding import PartitionSpec as P

BLOCK = 128


def contract_rows(left, right):
    return lax.dot_general(
        left, right, (((0,), (0,)), ((), ())), preferred_element_type=jnp.float32
    )


def contract_cols(left, right):
    return lax.dot_general(
        left, right, (((1,), (1,)), ((), ())), preferred_element_type=jnp.float32
    )


def per_device(eigvecs, reflectors, factors, frequencies, region_blocks):
    highest = lax.Precision.HIGHEST
    first_block = reflectors[0]
    second_block = reflectors[1]
    first_factor = jnp.triu(factors[0])
    second_factor = jnp.triu(factors[1])
    second_local = contract_rows(second_block, eigvecs)
    first_local = contract_rows(first_block, eigvecs)
    cross_local = contract_rows(first_block, second_block)
    second_proj, first_part, cross = lax.psum((second_local, first_local, cross_local), "row")
    second_apply = jnp.dot(second_factor, second_proj, precision=highest).astype(jnp.bfloat16)
    first_proj = first_part - jnp.dot(cross, second_apply.astype(jnp.float32), precision=highest)
    first_apply = jnp.dot(first_factor, first_proj, precision=highest).astype(jnp.bfloat16)
    local_blocks = eigvecs.shape[0] // BLOCK
    columns = eigvecs.shape[1]
    width = reflectors.shape[2]
    local_index = region_blocks - lax.axis_index("row") * local_blocks
    picked_vecs = jnp.take(
        eigvecs.reshape(local_blocks, BLOCK, columns), local_index, axis=0
    ).reshape(-1, columns)
    picked_refl = jnp.take(
        reflectors.reshape(2, local_blocks, BLOCK, width), local_index, axis=1
    ).reshape(2, -1, width)
    region = picked_vecs.astype(jnp.float32)
    region = region - jnp.dot(picked_refl[1], second_apply, preferred_element_type=jnp.float32)
    region = region - jnp.dot(picked_refl[0], first_apply, preferred_element_type=jnp.float32)
    region = region.astype(jnp.bfloat16)
    weight_all = 1.0 / jnp.tanh(frequencies / 2.0) / (2.0 * frequencies)
    column_index = lax.axis_index("col")
    weight = lax.dynamic_slice_in_dim(weight_all, column_index * columns, columns, 0)
    scaled = (region.astype(jnp.float32) * weight[None, :]).astype(jnp.bfloat16)
    whole = lax.all_gather(region, "row", axis=0, tiled=True)
    partner = lax.all_to_all(whole, "col", split_axis=0, concat_axis=1, tiled=True)
    return contract_cols(lax.all_gather(scaled, "col", axis=1, tiled=True), partner)


def solution(mesh):
    return jax.shard_map(
        per_device,
        mesh=mesh,
        in_specs=(P("row", "col"), P(None, "row", None), P(), P(), P("row")),
        out_specs=P("row", "col"),
        check_vma=False,
    )
```

profile of v0, /device:TPU:0, one launch (start us, length us, event | category | flops | bytes accessed | tf_op | source)
XLA Modules:
  0.0 279.0 jit_solution(16794748032254373549)
XLA Ops:
  6.5 0.0 all-reduce.3.cloned.1.call-start
  6.5 0.0 copy-start
  6.5 4.2 %fusion.1 = f32[128,128]{1,0:T(8,128)} fusion(bf16[2,10240,128]{2,1,0:T(8,128)(2,1)} %param.6), kind=kOutput, calls=%fused_computation.5 | convolution fusion | flops 335544320 | bytes 5308416 | tf_op jit(solution)/shard_map/dot_general | solution.py:10
  10.7 0.0 copy-done
  10.7 3.7 %fusion.3 = f32[128,256]{1,0:T(8,128)} fusion(bf16[10240,256]{1,0:T(8,128)(2,1)S(1)} %copy-done, bf16[2,10240,128]{2,1,0:T(8,128)(2,1)} %param.6), kind=kOutput, calls=%fused_computation.7 | convolution fusion | flops 671088640 | bytes 7995392 | tf_op jit(solution)/shard_map/dot_general | solution.py:10
  14.4 0.0 slice-done
  14.4 0.0 slice-done.1
  14.4 1.7 fusion.6
  16.1 0.0 all-reduce.3.cloned.1.call-update
  16.1 0.0 all-gather.5.cloned.1.call-start
  16.2 0.0 copy-done.1
  16.2 0.1 broadcast_bitcast_fusion
  16.3 3.3 %gather_fusion.1 = bf16[18,2,128,128]{3,2,1,0:T(8,128)(2,1)S(1)} fusion(bf16[2,80,128,128]{3,2,1,0:T(8,128)(2,1)} %bitcast.43, s32[1024]{0:T(1024)S(1)} %pad_clamp_fusion), kind=kCustom, calls=%fused_computation.1 | custom fusion | bytes 2359368 | tf_op jit(solution)/shard_map/jit(_take)/gather | solution.py:41
  19.6 0.2 select_bitcast_fusion
  19.8 3.1 %gather_fusion = bf16[18,128,256]{2,1,0:T(8,128)(2,1)S(1)} fusion(bf16[80,128,256]{2,1,0:T(8,128)(2,1)} %bitcast.42, s32[1024]{0:T(1024)S(1)} %pad_clamp_fusion), kind=kCustom, calls=%fused_computation | custom fusion | bytes 2359368 | tf_op jit(solution)/shard_map/jit(_take)/gather | solution.py:38
  22.9 0.8 multiply_divide_fusion
  23.6 1.2 bitcast_select_fusion
  24.9 0.1 fusion.20
  25.0 30.7 %all-reduce.3.cloned.1.call-done = (f32[128,256]{1,0:T(8,128)}, f32[128,256]{1,0:T(8,128)}, f32[128,128]{1,0:T(8,128)}) async-done(((f32[128,256]{1,0:T(8,128)}, f32[128,256]{1,0:T(8,128)}, f32[128,128]{1,0:T(8,128)}), (f32[128,256]{1,0:T(8,128)}, f32[128,256]{1,0:T(8,128)}, f32[128,128]{1,0:T(8,128)})) %all-reduce.3.cloned.1.call-update) | async-done | bytes 327696 | tf_op jit(solution)/shard_map/psum | solution.py:30
  55.7 1.3 convolution_convert_fusion.1
  56.9 1.1 convolution_subtract_fusion.2
  58.1 1.2 convolution_convert_fusion
  59.2 0.4 convolution_subtract_fusion.1
  59.7 1.9 multiply_convert_fusion
  61.5 0.0 all-gather.5.cloned.1.call-update
  61.6 0.0 all-gather.3.cloned.1.call-start
  61.6 0.7 all-gather.3.cloned.1.call-update
  62.3 88.5 %all-gather.5.cloned.1.call-done = bf16[9216,256]{1,0:T(8,128)(2,1)} async-done(((bf16[2304,256]{1,0:T(8,128)(2,1)}), bf16[9216,256]{1,0:T(8,128)(2,1)}) %all-gather.5.cloned.1.call-update) | async-done | bytes 4718608 | tf_op jit(solution)/shard_map/all_gather | solution.py:52
  150.8 6.6 %copy.6 = bf16[8,1152,256]{1,2,0:T(8,128)(2,1)} copy(bf16[8,1152,256]{2,1,0:T(8,128)(2,1)} %bitcast.46) | data formatting | bytes 9437184 | tf_op jit(solution)/shard_map/all_to_all | solution.py:53
  157.4 85.1 %all_to_all.19 = bf16[8,1152,256]{1,2,0:T(8,128)(2,1)} all-to-all(bf16[8,1152,256]{1,2,0:T(8,128)(2,1)} %copy.6), channel_id=1, replica_groups=mesh['row'=4,'col'=8] {'col'}, dimensions={0} | all-to-all | bytes 9437184 | tf_op jit(solution)/shard_map/all_to_all | solution.py:53
  242.6 12.1 %all-gather.3.cloned.1.call-done = bf16[2304,2048]{1,0:T(8,128)(2,1)} async-done(((bf16[2304,256]{1,0:T(8,128)(2,1)}), bf16[2304,2048]{1,0:T(8,128)(2,1)}) %all-gather.3.cloned.1.call-update) | async-done | bytes 9437200 | tf_op jit(solution)/shard_map/all_gather | solution.py:54
  254.7 17.8 %fusion.21 = f32[2304,1152]{1,0:T(8,128)} fusion(bf16[2304,2048]{1,0:T(8,128)(2,1)} %all-gather.3.cloned.1.call-done, bf16[1152,2048]{0,1:T(8,128)(2,1)} %bitcast.47), kind=kOutput, calls=%fused_computation.40 | convolution fusion | flops 10871635968 | bytes 24772608 | tf_op jit(solution)/shard_map/dot_general | solution.py:16
  (7 shorter events, 0.0 us)
Async XLA Ops:
  6.5 49.1 %all-reduce.3.cloned.1.call-start = ((), (), s32[]{:S(2)}) async-start(), calls=%async_computation.3 | async-start | bytes 655360 | tf_op jit(solution)/shard_map/psum | solution.py:30
  6.5 4.2 %copy-start = (bf16[10240,256]{1,0:T(8,128)(2,1)S(1)}, bf16[10240,256]{1,0:T(8,128)(2,1)}, u32[]{:S(2)}) copy-start(bf16[10240,256]{1,0:T(8,128)(2,1)} %param.5) | copy-start | bytes 15728644
  6.5 7.9 %slice-start = ((s8[5242880]{0:T(1024)(128)(4,1)}), s8[4194304]{0:T(1024)(128)(4,1)S(1)}, s32[]{:S(2)}) async-start(s8[5242880]{0:T(1024)(128)(4,1)} %bitcast.44), calls=%async_computation.4 | async-start | bytes 8388608
  10.7 3.7 %slice-start.1 = ((s8[5242880]{0:T(1024)(128)(4,1)}), s8[1048576]{0:T(1024)(128)(4,1)S(1)}, s32[]{:S(2)}) async-start(s8[5242880]{0:T(1024)(128)(4,1)} %bitcast.44), calls=%async_computation.5 | async-start | bytes 2097152
  14.4 1.8 copy-start.1
  16.1 134.7 %all-gather.5.cloned.1.call-start = ((), (), s32[]{:S(2)}) async-start(), calls=%async_computation.2 | async-start | bytes 5898240 | tf_op jit(solution)/shard_map/all_gather | solution.py:52
  61.6 193.1 %all-gather.3.cloned.1.call-start = ((), (), s32[]{:S(2)}) async-start(), calls=%async_computation.1 | async-start | bytes 10616832 | tf_op jit(solution)/shard_map/all_gather | solution.py:54
Sparse Core Ops, SparseCore 0:
  16.3 39.3 all-reduce.2
  61.7 89.0 all-gather.4
  152.7 101.9 all-gather.2
where the time goes:
time: 279 us
  waiting for transfers between devices  132 us (47%)
  blocking collectives  85.1 us (31%)
  matrix products  33.2 us (12%)
  local copies, waits for them, and re-layouts  13.2 us (5%)
  between operations  13.2 us (5%)
    all_gather x1, waiting for transfers between devices, per_device(): whole = lax.all_gather(region, 'row', axis=0, tiled=True)  88.5 us
    all_to_all x1, blocking collectives, per_device(): lax.all_to_all(whole, 'col', split_axis=0, concat_axis=1, tiled=True)  85.1 us
    psum x1, waiting for transfers between devices, per_device(): lax.psum((second_local, first_local, cross_local), 'row')  30.7 us
    dot_general x1, matrix products, contract_cols(): lax.dot_general(left, right, (((1,), (1,)), ((), ())), preferred_element_...  17.8 us
    all_gather x1, waiting for transfers between devices, per_device(): lax.all_gather(scaled, 'col', axis=1, tiled=True)  12.1 us
    dot_general x3, matrix products, contract_rows(): lax.dot_general(left, right, (((0,), (0,)), ((), ())), preferred_element_...  9.56 us
    all_to_all x1, local copies, waits for them, and re-layouts, per_device(): lax.all_to_all(whole, 'col', split_axis=0, concat_axis=1, tiled=True)  6.62 us
  transfers between devices with their start and end apart: 3, of which 3 were waited for; matrix products, arithmetic and copies ran while one was open for 6% of the time, Pallas kernels for 0%

commit v1 on v0

--- a/solution.py
+++ b/solution.py
@@ -49,7 +49,12 @@
     column_index = lax.axis_index("col")
     weight = lax.dynamic_slice_in_dim(weight_all, column_index * columns, columns, 0)
     scaled = (region.astype(jnp.float32) * weight[None, :]).astype(jnp.bfloat16)
-    whole = lax.all_gather(region, "row", axis=0, tiled=True)
+    ring = [region]
+    for hop in range(3):
+        ring.append(lax.ppermute(ring[-1], "row", [(dev, (dev + 1) % 4) for dev in range(4)]))
+    whole = jnp.roll(
+        jnp.concatenate(ring[::-1], axis=0), (lax.axis_index("row") + 1) * ring[0].shape[0], axis=0
+    )
     partner = lax.all_to_all(whole, "col", split_axis=0, concat_axis=1, tiled=True)
     return contract_cols(lax.all_gather(scaled, "col", axis=1, tiled=True), partner)
 

time: 279 us -> 238 us (0.85)
  blocking collectives: 85.1 us -> 59.4 us
  waiting for transfers between devices: 132 us -> 109 us
  local copies, waits for them, and re-layouts: 13.2 us -> 17.7 us
    all_gather x1 -> x0, waiting for transfers between devices: 88.5 us -> none  [per_device(): whole = lax.all_gather(region, 'row', axis=0, tiled=True)]
    ppermute x0 -> x3, waiting for transfers between devices: none -> 78.8 us  [per_device(): lax.ppermute(ring[-1], 'row', [(dev, (dev + 1) % 4) for dev in range(4)])]
    all_to_all x1, blocking collectives: 85.1 us -> 59.4 us  [per_device(): lax.all_to_all(whole, 'col', split_axis=0, concat_axis=1, tiled=True)]
    all_gather x1, waiting for transfers between devices: 12.1 us -> 0.01 us  [per_device(): lax.all_gather(scaled, 'col', axis=1, tiled=True)]
    unnamed x8 -> x15, local copies, waits for them, and re-layouts: 0.01 us -> 3.1 us
  transfers between devices with their start and end apart: 3 -> 5, of which waited for: 3 -> 4; matrix products, arithmetic and copies ran while one was open for 6% -> 8% of each run, Pallas kernels for 0% -> 0%
where the time goes in v1:
time: 238 us; the launch traced here: 237 us
  waiting for transfers between devices  109 us (46%)
  blocking collectives  59.4 us (25%)
  matrix products  33.5 us (14%)
  local copies, waits for them, and re-layouts  17.7 us (7%)
  between operations  13.6 us (6%)
    ppermute x3, waiting for transfers between devices, per_device(): lax.ppermute(ring[-1], 'row', [(dev, (dev + 1) % 4) for dev in range(4)])  78.8 us
    all_to_all x1, blocking collectives, per_device(): lax.all_to_all(whole, 'col', split_axis=0, concat_axis=1, tiled=True)  59.4 us
    psum x1, waiting for transfers between devices, per_device(): lax.psum((second_local, first_local, cross_local), 'row')  30.6 us
    dot_general x1, matrix products, contract_cols(): lax.dot_general(left, right, (((1,), (1,)), ((), ())), preferred_element_...  17.8 us
    dot_general x3, matrix products, contract_rows(): lax.dot_general(left, right, (((0,), (0,)), ((), ())), preferred_element_...  10.2 us
    all_to_all x1, local copies, waits for them, and re-layouts, per_device(): lax.all_to_all(whole, 'col', split_axis=0, concat_axis=1, tiled=True)  6.73 us
  transfers between devices with their start and end apart: 5, of which 4 were waited for; matrix products, arithmetic and copies ran while one was open for 8% of the time, Pallas kernels for 0%

profile of v1, /device:TPU:0, one launch (start us, length us, event | category | flops | bytes accessed | tf_op | source)
XLA Modules:
  0.0 237.4 jit_solution(4860137053352380429)
XLA Ops:
  6.5 5.1 %fusion.3 = f32[128,256]{1,0:T(8,128)} fusion(bf16[10240,256]{1,0:T(8,128)(2,1)} %param.5, bf16[2,10240,128]{2,1,0:T(8,128)(2,1)} %param.6), kind=kOutput, calls=%fused_computation.7 | convolution fusion | flops 671088640 | bytes 7995392 | tf_op jit(solution)/shard_map/dot_general | solution.py:10
  11.6 3.6 %fusion.6 = f32[128,256]{1,0:T(8,128)} fusion(bf16[10240,256]{1,0:T(8,128)(2,1)S(1)} %copy-done, bf16[2,10240,128]{2,1,0:T(8,128)(2,1)} %param.6), kind=kOutput, calls=%fused_computation.10 | convolution fusion | flops 671088640 | bytes 7995392 | tf_op jit(solution)/shard_map/dot_general | solution.py:10
  15.3 1.5 fusion.1
  16.9 0.1 broadcast_bitcast_fusion
  17.0 3.3 %gather_fusion.1 = bf16[18,2,128,128]{3,2,1,0:T(8,128)(2,1)S(1)} fusion(bf16[2,80,128,128]{3,2,1,0:T(8,128)(2,1)} %bitcast.44, s32[1024]{0:T(1024)S(1)} %pad_clamp_fusion), kind=kCustom, calls=%fused_computation.1 | custom fusion | bytes 2359368 | tf_op jit(solution)/shard_map/jit(_take)/gather | solution.py:41
  20.3 0.2 select_bitcast_fusion
  20.4 3.1 %gather_fusion = bf16[18,128,256]{2,1,0:T(8,128)(2,1)S(1)} fusion(bf16[80,128,256]{2,1,0:T(8,128)(2,1)} %bitcast.41, s32[1024]{0:T(1024)S(1)} %pad_clamp_fusion), kind=kCustom, calls=%fused_computation | custom fusion | bytes 2359368 | tf_op jit(solution)/shard_map/jit(_take)/gather | solution.py:38
  23.6 1.2 bitcast_select_fusion
  24.8 0.8 multiply_divide_fusion
  25.6 0.1 fusion.20
  25.7 30.6 %all-reduce.3.cloned.1.call-done = (f32[128,256]{1,0:T(8,128)}, f32[128,256]{1,0:T(8,128)}, f32[128,128]{1,0:T(8,128)}) async-done(((f32[128,256]{1,0:T(8,128)}, f32[128,256]{1,0:T(8,128)}, f32[128,128]{1,0:T(8,128)}), (f32[128,256]{1,0:T(8,128)}, f32[128,256]{1,0:T(8,128)}, f32[128,128]{1,0:T(8,128)})) %all-reduce.3.cloned.1.call-update) | async-done | bytes 327696 | tf_op jit(solution)/shard_map/psum | solution.py:30
  56.3 1.3 convolution_convert_fusion.1
  57.6 1.1 convolution_subtract_fusion.2
  58.7 1.2 convolution_convert_fusion
  59.9 0.4 convolution_subtract_fusion.1
  60.3 1.5 multiply_convert_fusion
  61.8 1.5 collective-permute-start
  63.4 26.1 %collective-permute-done = bf16[2304,256]{1,0:T(8,128)(2,1)S(1)} collective-permute-done((bf16[2304,256]{1,0:T(8,128)(2,1)S(1)}, bf16[2304,256]{1,0:T(8,128)(2,1)S(1)}, u32[]{:S(2)}, u32[]{:S(2)}) %collective-permute-start) | collective-permute-done | bytes 1179680 | tf_op jit(solution)/shard_map/ppermute | solution.py:54
  89.5 26.7 %collective-permute-done.1 = bf16[2304,256]{1,0:T(8,128)(2,1)S(1)} collective-permute-done((bf16[2304,256]{1,0:T(8,128)(2,1)S(1)}, bf16[2304,256]{1,0:T(8,128)(2,1)S(1)}, u32[]{:S(2)}, u32[]{:S(2)}) %collective-permute-start.1) | collective-permute-done | bytes 1179680 | tf_op jit(solution)/shard_map/ppermute | solution.py:54
  116.2 26.0 %collective-permute-done.2 = bf16[2304,256]{1,0:T(8,128)(2,1)} collective-permute-done((bf16[2304,256]{1,0:T(8,128)(2,1)S(1)}, bf16[2304,256]{1,0:T(8,128)(2,1)}, u32[]{:S(2)}, u32[]{:S(2)}) %collective-permute-start.2) | collective-permute-done | bytes 1179680 | tf_op jit(solution)/shard_map/ppermute | solution.py:54
  142.2 1.3 constant_dynamic-update-slice_fusion.7
  143.5 0.1 constant_dynamic-update-slice_fusion.6
  143.6 0.1 constant_dynamic-update-slice_fusion.5
  143.7 0.1 constant_dynamic-update-slice_fusion.4
  143.8 1.3 constant_dynamic-update-slice_fusion.3
  145.2 0.1 constant_dynamic-update-slice_fusion.2
  145.2 0.1 constant_dynamic-update-slice_fusion.1
  145.3 0.1 constant_dynamic-update-slice_fusion
  145.4 1.2 constant_dynamic-slice_fusion
  146.7 59.4 %all_to_all.19 = bf16[8,1152,256]{2,1,0:T(8,128)(2,1)} all-to-all(bf16[8,1152,256]{2,1,0:T(8,128)(2,1)S(1)} %bitcast.42), channel_id=1, replica_groups=mesh['row'=4,'col'=8] {'col'}, dimensions={0} | all-to-all | bytes 9437184 | tf_op jit(solution)/shard_map/all_to_all | solution.py:58
  206.1 6.7 %copy.6 = bf16[1152,8,256]{0,2,1:T(8,128)(2,1)} copy(bf16[1152,8,256]{2,0,1:T(8,128)(2,1)} %bitcast.43) | data formatting | bytes 9437184 | tf_op jit(solution)/shard_map/all_to_all | solution.py:58
  212.8 17.8 %fusion.21 = f32[2304,1152]{1,0:T(8,128)} fusion(bf16[2304,2048]{1,0:T(8,128)(2,1)} %all-gather.2.cloned.1.call-done, bf16[1152,2048]{0,1:T(8,128)(2,1)} %bitcast.47), kind=kOutput, calls=%fused_computation.49 | convolution fusion | flops 10871635968 | bytes 24772608 | tf_op jit(solution)/shard_map/dot_general | solution.py:16
  (19 shorter events, 0.1 us)
Async XLA Ops:
  6.5 49.8 %all-reduce.3.cloned.1.call-start = ((), (), s32[]{:S(2)}) async-start(), calls=%async_computation.2 | async-start | bytes 655360 | tf_op jit(solution)/shard_map/psum | solution.py:30
  6.5 5.1 %copy-start = (bf16[10240,256]{1,0:T(8,128)(2,1)S(1)}, bf16[10240,256]{1,0:T(8,128)(2,1)}, u32[]{:S(2)}) copy-start(bf16[10240,256]{1,0:T(8,128)(2,1)} %param.5) | copy-start | bytes 15728644
  6.5 8.7 %slice-start = ((s8[5242880]{0:T(1024)(128)(4,1)}), s8[4194304]{0:T(1024)(128)(4,1)S(1)}, s32[]{:S(2)}) async-start(s8[5242880]{0:T(1024)(128)(4,1)} %bitcast.45), calls=%async_computation.3 | async-start | bytes 8388608
  11.6 3.6 %slice-start.1 = ((s8[5242880]{0:T(1024)(128)(4,1)}), s8[1048576]{0:T(1024)(128)(4,1)S(1)}, s32[]{:S(2)}) async-start(s8[5242880]{0:T(1024)(128)(4,1)} %bitcast.45), calls=%async_computation.4 | async-start | bytes 2097152
  15.3 1.6 copy-start.1
  16.8 196.0 %all-gather.2.cloned.1.call-start = ((), (), s32[]{:S(2)}) async-start(), calls=%async_computation.1 | async-start | bytes 10616832 | tf_op jit(solution)/shard_map/all_gather | solution.py:59
  61.8 27.6 %collective-permute-start = (bf16[2304,256]{1,0:T(8,128)(2,1)S(1)}, bf16[2304,256]{1,0:T(8,128)(2,1)S(1)}, u32[]{:S(2)}, u32[]{:S(2)}) collective-permute-start(bf16[2304,256]{1,0:T(8,128)(2,1)S(1)} %get-tuple-element.13), channel_id=1, source_target_pairs={{0,8},{8,16},{16,24},{24,0},{1,9},{9,17},{17,25},{25,1},{2,10},{10... | collective-permute-start | bytes 3538952 | tf_op jit(solution)/shard_map/ppermute | solution.py:54
  89.5 26.7 %collective-permute-start.1 = (bf16[2304,256]{1,0:T(8,128)(2,1)S(1)}, bf16[2304,256]{1,0:T(8,128)(2,1)S(1)}, u32[]{:S(2)}, u32[]{:S(2)}) collective-permute-start(bf16[2304,256]{1,0:T(8,128)(2,1)S(1)} %collective-permute-done), channel_id=1, source_target_pairs={{0,8},{8,16},{16,24},{24,0},{1,9},{9,17},{17,25},{25,1},{2,10},{10... | collective-permute-start | bytes 3538952 | tf_op jit(solution)/shard_map/ppermute | solution.py:54
  116.2 26.0 %collective-permute-start.2 = (bf16[2304,256]{1,0:T(8,128)(2,1)S(1)}, bf16[2304,256]{1,0:T(8,128)(2,1)}, u32[]{:S(2)}, u32[]{:S(2)}) collective-permute-start(bf16[2304,256]{1,0:T(8,128)(2,1)S(1)} %collective-permute-done.1), channel_id=1, source_target_pairs={{0,8},{8,16},{16,24},{24,0},{1,9},{9,17},{17,25},{25,1},{2,10},{10... | collective-permute-start | bytes 3538952 | tf_op jit(solution)/shard_map/ppermute | solution.py:54
Sparse Core Ops, SparseCore 0:
  16.9 39.3 all-reduce.2
  62.0 60.1 all-gather.1
